TPU v7x, 32 devices: a whole 2x2x4 slice. The times are simulated.
32 devices in a mesh: strip: 8 (over z, x), col: 4 (over y, core).
Axes of the slice: x: 2, y: 2, z: 4, core: 2. Of those that a mesh axis runs over, the one named last changes fastest.
Arguments:
- residuals: float32 [16, 64, 2560], P('strip'), may hold values from -6 to 6
- corr_rows: float32 [64], replicated, may hold values from 0.5 to 2
- corr_cols: float32 [2560], replicated, may hold values from 0.5 to 2
- row_anchor: int32 [16], replicated, may hold values from 0 to 64
- col_anchor: int32 [16], replicated, may hold values from 0 to 7680
- valid_first: int32 [16], replicated, may hold values from 0 to 15
- valid_end: int32 [16], replicated, may hold values from 49 to 64
- facet_of_slot: int32 [16], replicated, may hold values from 0 to 15, each once
Outputs:
- stitched: float32 [128, 10240], P('strip', 'col')
- column_power: float32 [10240], P('col')
Inputs may be any that keep to these rules, and one draw needn't show every extreme that they name: facet_of_slot names each of the 16 facets exactly once.
All inputs are finite; a program needn't handle non-finite values.
Results may differ from a plain program's by a relative error of at most 0.0003.
Values sent between devices are 32-bit elements; how exact they have to be, the bound alone decides.
A program may use at most 64 MiB of HBM per device.

v0:
```python
import jax
import jax.numpy as jnp
from jax import lax
from jax.sharding import PartitionSpec as P


def tapers(count):
    position = (jnp.arange(count).astype(jnp.float32) + 0.5) / count
    return jnp.sin(jnp.pi * position) ** 2


def body(
    residuals, corr_rows, corr_cols, row_anchor, col_anchor, valid_first, valid_end, facet_of_slot
):
    local_count, facet_rows, facet_cols = residuals.shape
    strip_count = lax.axis_size("strip")
    strip_rows = facet_rows // 4
    image_rows = strip_count * strip_rows
    strip_index = lax.axis_index("strip")
    group_index = lax.axis_index("col")
    row_index = jnp.arange(facet_rows)
    row_taper = tapers(facet_rows)
    col_taper = tapers(facet_cols)
    correction = corr_rows[:, None] * corr_cols[None, :]
    side_blank = jnp.zeros((facet_rows, facet_cols), jnp.float32)
    num_bands = []
    for position in range(local_count):
        facet_id = facet_of_slot[strip_index * local_count + position]
        inside = (row_index >= valid_first[facet_id]) & (row_index < valid_end[facet_id])
        row_weight = jnp.where(inside, row_taper, 0.0)
        weight = row_weight[:, None] * col_taper[None, :]
        col_start = jnp.clip(
            group_index * facet_cols - col_anchor[facet_id] + facet_cols, 0, 2 * facet_cols
        )
        padded = jnp.concatenate(
            [side_blank, weight * correction * residuals[position], side_blank], axis=1
        )
        shifted = lax.dynamic_slice_in_dim(padded, col_start, facet_cols, 1)
        canvas = jnp.zeros((image_rows, facet_cols), jnp.float32)
        canvas = lax.dynamic_update_slice(canvas, shifted, (row_anchor[facet_id], 0))
        num_bands.append(canvas.reshape(strip_count, strip_rows, facet_cols))
    num_send = jnp.stack(num_bands, axis=1)
    got_num = lax.all_to_all(num_send, "strip", split_axis=0, concat_axis=0, tiled=True)
    facet_ids = jnp.arange(facet_of_slot.shape[0])
    row_local = strip_index * strip_rows + jnp.arange(strip_rows)
    row_pos = row_local[None, :] - row_anchor[:, None]
    row_inside = (row_pos >= valid_first[:, None]) & (row_pos < valid_end[:, None])
    row_value = jnp.sin(jnp.pi * (row_pos.astype(jnp.float32) + 0.5) / facet_rows) ** 2
    row_part = jnp.where(row_inside, row_value, 0.0)
    col_local = group_index * facet_cols + jnp.arange(facet_cols)
    col_pos = col_local[None, :] - col_anchor[facet_ids][:, None]
    col_inside = (col_pos >= 0) & (col_pos < facet_cols)
    col_value = jnp.sin(jnp.pi * (col_pos.astype(jnp.float32) + 0.5) / facet_cols) ** 2
    col_part = jnp.where(col_inside, col_value, 0.0)
    denominator = jnp.einsum("fv,fu->vu", row_part, col_part, precision=lax.Precision.HIGHEST)
    numerator = jnp.sum(got_num, axis=(0, 1))
    stitched = numerator / jnp.maximum(denominator, 0.5)
    column_sums = lax.psum(jnp.sum(stitched * stitched, axis=0), "strip")
    return (stitched, column_sums / image_rows)


def solution(mesh):
    in_specs = (P("strip", None, None), P(), P(), P(), P(), P(), P(), P())
    out_specs = (P("strip", "col"), P("col"))
    return jax.shard_map(body, mesh=mesh, in_specs=in_specs, out_specs=out_specs, check_vma=False)
```

profile of v0, /device:TPU:0, one launch (start us, length us, event | category | flops | bytes accessed | tf_op | source)
XLA Modules:
  0.0 127.9 jit_solution(10135443065391539872)
XLA Ops:
  0.6 1.3 %fusion.47 = (s32[1]{0:T(128)}, s32[1]{0:T(128)}) fusion(s32[16]{0:T(128)} %param.15, s32[]{:T(128)S(6)} %select_n.50, s32[]{:T(128)S(6)} %select_n.54), kind=kLoop, calls=%fused_computation.69 | loop fusion | bytes 24 | tf_op jit(solution)/shard_map/dynamic_slice | solution.py:28
  4.6 0.1 sine_multiply_fusion
  5.9 1.4 %fusion.43 = (s32[1]{0:T(128)}, s32[1]{0:T(128)}, s32[1]{0:T(128)}, s32[1]{0:T(128)}) fusion(s32[16]{0:T(128)} %param.11, s32[]{:T(128)S(6)} %select_n.51, s32[]{:T(128)S(6)} %select_n.55, s32[16]{0:T(128)} %param.13), kind=kLoop, calls=%fused_computation.65 | loop fusion | bytes 40 | tf_op jit(solution)/shard_map/dynamic_slice | solution.py:40
  9.8 1.4 %fusion.45 = (s32[1]{0:T(128)}, s32[1]{0:T(128)}, s32[1]{0:T(128)}, s32[1]{0:T(128)}) fusion(s32[16]{0:T(128)} %param.14, s32[]{:T(128)S(6)} %select_n.51, s32[]{:T(128)S(6)} %select_n.55, s32[16]{0:T(128)} %param.12), kind=kLoop, calls=%fused_computation.67 | loop fusion | bytes 40 | tf_op jit(solution)/shard_map/dynamic_slice | solution.py:29
  12.5 1.2 and_select_fusion
  13.7 1.4 %and_select_fusion.1 = f32[64]{0:T(128)S(1)} fusion(s32[]{:T(128)} %bitcast.2, s32[]{:T(128)} %bitcast.1), kind=kLoop, calls=%fused_computation.56 | loop fusion | flops 512 | bytes 264 | tf_op jit(solution)/shard_map/jit(_where)/select_n | solution.py:30
  16.3 1.5 %fusion.1 = (f32[64,2560]{1,0:T(8,128)S(1)}, f32[64,2560]{1,0:T(8,128)S(1)}) fusion(f32[2,64,2560]{2,1,0:T(8,128)} %param.8, f32[2560]{0:T(1024)} %param.10, f32[64]{0:T(128)} %param.9, f32[2560]{0:T(1024)S(1)} %sine_multiply_fusion, f32[64]{0:T(128)S(1)} %and_select_fusion.1, f32[64]{0:T(128)S(1)} %and_select_fusion), kind=kLoop, calls=%fused_computation.12 | loop fusion | flops 1146880 | bytes 2642688 | tf_op jit(solution)/shard_map/mul | solution.py:36
  17.9 1.1 fusion.6
  19.0 0.1 broadcast.78.clone.1
  19.2 1.2 dynamic_update_slice.6
  20.3 0.1 broadcast.78.clone
  20.5 1.2 dynamic_update_slice.7
  21.7 1.7 %pad_maximum_fusion = f32[8,2,16,2560]{3,2,1,0:T(8,128)} fusion(f32[8,1,16,2560]{3,2,1,0:T(8,128)S(1)} %bitcast.16, f32[8,1,16,2560]{3,2,1,0:T(8,128)S(1)} %bitcast.17), kind=kLoop, calls=%fused_computation.7 | loop fusion | flops 655360 | bytes 5242880 | tf_op jit(solution)/shard_map/stack | solution.py:42
  23.4 7.4 %all-to-all-start = ((f32[8,2,16,2560]{3,2,1,0:T(8,128)}), f32[8,2,16,2560]{3,2,1,0:T(8,128)S(1)}, u32[]{:S(2)}, u32[]{:S(2)}) async-start(f32[8,2,16,2560]{3,2,1,0:T(8,128)} %pad_maximum_fusion), calls=%async_computation | async-start | bytes 5242880 | tf_op jit(solution)/shard_map/all_to_all | solution.py:43
  30.8 0.0 copy-start.2
  30.8 0.0 copy-start.3
  30.9 0.7 gather_fusion
  31.6 58.7 %all-to-all-done = f32[8,2,16,2560]{3,2,1,0:T(8,128)S(1)} async-done(((f32[8,2,16,2560]{3,2,1,0:T(8,128)}), f32[8,2,16,2560]{3,2,1,0:T(8,128)S(1)}, u32[]{:S(2)}, u32[]{:S(2)}) %all-to-all-start) | async-done | bytes 2621472 | tf_op jit(solution)/shard_map/all_to_all | solution.py:43
  90.3 0.1 reduce_sum.18
  90.4 0.0 copy-done.1
  90.4 0.0 copy-done.2
  90.5 1.6 %multiply_reduce_fusion = (f32[2560]{0:T(1024)S(1)}, f32[16,2560]{1,0:T(8,128)}) fusion(f32[16,2560]{1,0:T(8,128)S(1)} %reduce_sum.18, s32[16]{0:T(128)S(1)} %gather_fusion, s32[2560]{0:T(1024)S(1)} %iota_add_fusion, s32[16]{0:T(128)S(1)} %copy-done.1, s32[16]{0:T(128)S(1)} %copy-done.3, s32[16]{0:T(128)S(1)} %copy-done.2, s32[16]{0:T(128)S(1)} %iota_add_fusion.1), kind=kOutput, calls=%fused_computation.26 | convolution fusion | flops 8396544 | bytes 348480 | tf_op jit(solution)/shard_map/fv,fu->vu/dot_general | solution.py:55
  92.1 35.2 %psum.7 = f32[2560]{0:T(1024)S(1)} all-reduce(f32[2560]{0:T(1024)S(1)} %get-tuple-element.16), channel_id=1, replica_groups=mesh['strip'=8,'col'=4] {'strip'}, use_global_device_ids=true, to_apply=%region_2.3 | all-reduce | flops 2560 | bytes 20480 | tf_op jit(solution)/shard_map/psum | solution.py:58
  127.3 0.6 broadcast_multiply_fusion
  (9 shorter events, 0.1 us)
Async XLA Ops:
  23.4 7.5 %copy-start = (s32[16]{0:T(128)S(1)}, s32[16]{0:T(128)}, u32[]{:S(2)}) copy-start(s32[16]{0:T(128)} %param.12) | copy-start | bytes 196
  23.4 66.9 %all-to-all-start = ((f32[8,2,16,2560]{3,2,1,0:T(8,128)}), f32[8,2,16,2560]{3,2,1,0:T(8,128)S(1)}, u32[]{:S(2)}, u32[]{:S(2)}) async-start(f32[8,2,16,2560]{3,2,1,0:T(8,128)} %pad_maximum_fusion), calls=%async_computation | async-start | bytes 5242880 | tf_op jit(solution)/shard_map/all_to_all | solution.py:43
  30.8 59.6 %copy-start.1 = (s32[16]{0:T(128)S(1)}, s32[16]{0:T(128)}, u32[]{:S(2)}) copy-start(s32[16]{0:T(128)} %param.14) | copy-start | bytes 196
  30.8 59.6 %copy-start.2 = (s32[16]{0:T(128)S(1)}, s32[16]{0:T(128)}, u32[]{:S(2)}) copy-start(s32[16]{0:T(128)} %param.11) | copy-start | bytes 196
  30.8 59.6 %copy-start.3 = (s32[16]{0:T(128)S(1)}, s32[16]{0:T(128)}, u32[]{:S(2)}) copy-start(s32[16]{0:T(128)} %param.13) | copy-start | bytes 196
where the time goes:
time: 128 us
  waiting for transfers between devices  58.7 us (46%)
  blocking collectives  35.2 us (28%)
  between operations  9.63 us (8%)
  other arithmetic  7.82 us (6%)
  local copies, waits for them, and re-layouts  7.47 us (6%)
  starting transfers between devices  7.41 us (6%)
  matrix products  1.64 us (1%)
    all_to_all x1, waiting for transfers between devices, body(): lax.all_to_all(num_send, 'strip', split_axis=0, concat_axis=0, tiled=True)  58.7 us
    psum x1, blocking collectives, body(): column_sums = lax.psum(jnp.sum(stitched * stitched, axis=0), 'strip')  35.2 us
    all_to_all x1, starting transfers between devices, body(): lax.all_to_all(num_send, 'strip', split_axis=0, concat_axis=0, tiled=True)  7.41 us
    select_n x2, other arithmetic, body(): row_weight = jnp.where(inside, row_taper, 0.0)  2.63 us
  transfers between devices with their start and end apart: 1, of which 1 were waited for; matrix products, arithmetic and copies ran while one was open for 1% of the time, Pallas kernels for 0%

commit v1 on v0

v1 whole, which is shorter than its diff:
```python
import functools
import math

import jax
import jax.numpy as jnp
from jax import lax
from jax.experimental import pallas as pl
from jax.experimental.pallas import tpu as pltpu
from jax.sharding import PartitionSpec as P

MESH = pl.DeviceIdType.MESH
CHUNKS = 2


def taper(position, count):
    angle = (position.astype(jnp.float32) + (0.5 - count / 2)) * (math.pi / count)
    square = angle * angle
    value = jnp.full_like(square, 1.0 / math.factorial(12))
    for order in (10, 8, 6, 4, 2, 0):
        sign = -1.0 if order % 4 == 2 else 1.0
        value = value * square + sign / math.factorial(order)
    return value * value


def visit_order(count):
    return [sorted(range(count), key=lambda d: (-abs(d - z), d < z)) for z in range(count)]


def place_kernel(
    strips, lanes, fid_ref, ra_ref, ca_ref, vf_ref, ve_ref, rows_ref, cols_ref, res_ref,
    blocks_ref, placed,
):
    local, fh, fw = res_ref.shape
    height = fh // 4
    width = fw // CHUNKS
    strip = lax.axis_index("strip")
    group = lax.axis_index("col")

    eye = lax.broadcasted_iota(jnp.int32, (fh, fh), 0) == lax.broadcasted_iota(
        jnp.int32, (fh, fh), 1
    )
    corr_row = jnp.sum(jnp.where(eye, rows_ref[...], 0.0), axis=1, keepdims=True)
    y = lax.broadcasted_iota(jnp.int32, (fh, 1), 0)
    u = lax.broadcasted_iota(jnp.int32, (1, fw), 1)
    row_taper = taper(y, fh)
    col_scale = taper(u, fw) * cols_ref[...]
    blank = jnp.zeros((height, fw), jnp.float32)
    sub = lax.broadcasted_iota(jnp.int32, (8, 1), 0)
    anchors = []
    for p in range(local):
        f = fid_ref[strip * local + p]
        ra, ca = ra_ref[f], ca_ref[f]
        anchors.append(ra)
        inside = (y >= vf_ref[f]) & (y < ve_ref[f])
        row_scale = jnp.where(inside, row_taper, 0.0) * corr_row
        col_pos = u + (group * fw - ca)
        col_inside = (col_pos >= 0) & (col_pos < fw)
        shift = lax.rem(ca, fw)
        lift = lax.rem(ra, 8)
        placed[p, pl.ds(0, height), :] = blank
        placed[p, pl.ds(height + fh + 8, height), :] = blank
        held = jnp.zeros((8, fw), jnp.float32)
        for row in range(0, fh, 8):
            term = res_ref[p, pl.ds(row, 8), :] * col_scale * row_scale[row : row + 8]
            term = jnp.where(col_inside, pltpu.roll(term, shift, axis=1), 0.0)
            term = pltpu.roll(term, lift, axis=0)
            placed[p, pl.ds(height + row, 8), :] = jnp.where(sub < lift, held, term)
            held = term
        placed[p, pl.ds(height + fh, 8), :] = jnp.where(sub < lift, held, 0.0)

    def place(block, chunk):
        total = None
        for p in range(local):
            tile = block * (height // 8) - lax.div(anchors[p], 8)
            start = (jnp.clip(tile, -height // 8, fh // 8 + 1) + height // 8) * 8
            start = pl.multiple_of(start, 8)
            part = placed[p, pl.ds(start, height), pl.ds(chunk * width, width)]
            total = part if total is None else total + part
        return total

    for block in range(strips):
        for c in range(CHUNKS):
            blocks_ref[block // lanes, block % lanes, c] = place(block, c)


def kernel(
    strips, lanes, ra_ref, ca_ref, vf_ref, ve_ref, blocks_ref,
    out_ref, power_ref, den, xrecv, zsend, zrecv, psend, precv,
    xs_sem, xr_sem, zs_sem, zr_sem, ps_sem, pr_sem,
):
    facets = ra_ref.shape[0]
    height, fw = out_ref.shape
    fh = 4 * height
    levels = strips // lanes
    width = fw // CHUNKS
    strip = lax.axis_index("strip")
    group = lax.axis_index("col")
    z, x = lax.div(strip, lanes), lax.rem(strip, lanes)

    barrier = pltpu.get_barrier_semaphore()
    for k in range(1, strips):
        peer = lax.rem(strip + k, strips)
        pl.semaphore_signal(barrier, inc=1, device_id={"strip": peer}, device_id_type=MESH)

    order = visit_order(levels)

    def dest(t):
        d = jnp.int32(order[0][t])
        for place_z in range(1, levels):
            d = jnp.where(z == place_z, jnp.int32(order[place_z][t]), d)
        return d

    def x_copy(k, d, c):
        return pltpu.make_async_remote_copy(
            src_ref=blocks_ref.at[d, lax.rem(x + k, lanes), c],
            dst_ref=xrecv.at[k - 1, d, c],
            send_sem=xs_sem.at[k - 1, d, c],
            recv_sem=xr_sem.at[k - 1, d, c],
            device_id={"strip": z * lanes + lax.rem(x + k, lanes)},
            device_id_type=MESH,
        )

    def z_copy(way, d, c, target):
        return pltpu.make_async_remote_copy(
            src_ref=zsend.at[d, c],
            dst_ref=zrecv.at[way, d, c],
            send_sem=zs_sem.at[d, c],
            recv_sem=zr_sem.at[way, d, c],
            device_id={"strip": target * lanes + x},
            device_id_type=MESH,
        )

    def p_copy(k):
        return pltpu.make_async_remote_copy(
            src_ref=psend,
            dst_ref=precv.at[k - 1],
            send_sem=ps_sem.at[k - 1],
            recv_sem=pr_sem.at[k - 1],
            device_id={"strip": lax.rem(strip + k, strips)},
            device_id_type=MESH,
        )

    pl.semaphore_wait(barrier, strips - 1)
    for t in range(levels):
        d = dest(t)
        for c in range(CHUNKS):
            for k in range(1, lanes):
                x_copy(k, d, c).start()

    v = lax.broadcasted_iota(jnp.int32, (height, 1), 0) + strip * height
    u8 = lax.broadcasted_iota(jnp.int32, (8, fw), 1) + group * fw

    den[...] = jnp.zeros_like(den)

    def add_facet(f, carry):
        row_pos = v - ra_ref[f]
        row_inside = (row_pos >= vf_ref[f]) & (row_pos < ve_ref[f])
        row_part = jnp.where(row_inside, taper(row_pos, fh), 0.0)
        col_pos = u8 - ca_ref[f]
        col_inside = (col_pos >= 0) & (col_pos < fw)
        col_part = jnp.where(col_inside, taper(col_pos, fw), 0.0)
        for row in range(0, height, 8):
            den[pl.ds(row, 8), :] += row_part[row : row + 8] * col_part
        return carry

    lax.fori_loop(0, facets, add_facet, 0)

    def gather_x(d, c):
        total = blocks_ref[d, x, c]
        for k in range(1, lanes):
            x_copy(k, d, c).wait_recv()
            total = total + xrecv[k - 1, d, c]
        return total

    for t in range(levels - 1):
        d = dest(t)
        right = d > z
        way = jnp.where(right, 0, 1)
        target = jnp.where(right, z + 1, z - 1)
        fed = jnp.where(right, z > 0, z < levels - 1)
        for c in range(CHUNKS):
            zsend[d, c] = gather_x(d, c)

            @pl.when(fed)
            def _():
                z_copy(way, d, c, target).wait_recv()
                zsend[d, c] += zrecv[way, d, c]

            z_copy(way, d, c, target).start()

    for c in range(CHUNKS):
        columns = pl.ds(c * width, width)
        out_ref[:, columns] = gather_x(z, c)

        @pl.when(z > 0)
        def _():
            z_copy(0, z, c, z - 1).wait_recv()
            out_ref[:, columns] += zrecv[0, z, c]

        @pl.when(z < levels - 1)
        def _():
            z_copy(1, z, c, z + 1).wait_recv()
            out_ref[:, columns] += zrecv[1, z, c]

        stitched = out_ref[:, columns] / jnp.maximum(den[:, columns], 0.5)
        out_ref[:, columns] = stitched
        psend[:, columns] = jnp.sum(stitched * stitched, axis=0, keepdims=True)

    for k in range(1, strips):
        p_copy(k).start()
    total = psend[...]
    for k in range(1, strips):
        p_copy(k).wait_recv()
        total = total + precv[k - 1]
    power_ref[...] = total * (1.0 / (strips * height))

    for k in range(1, strips):
        p_copy(k).wait_send()
    for t in range(levels):
        d = dest(t)
        for c in range(CHUNKS):
            for k in range(1, lanes):
                x_copy(k, d, c).wait_send()
            if t < levels - 1:
                z_copy(0, d, c, jnp.where(d > z, z + 1, z - 1)).wait_send()


def body(strips, lanes, residuals, corr_rows, corr_cols, row_anchor, col_anchor, first, end, slots):
    local, fh, fw = residuals.shape
    height = fh // 4
    levels = strips // lanes
    width = fw // CHUNKS
    others = max(lanes - 1, 1)
    smem = pl.BlockSpec(memory_space=pltpu.SMEM)
    vmem = pl.BlockSpec(memory_space=pltpu.VMEM)
    dma = pltpu.SemaphoreType.DMA
    block_bytes = 4 * height * fw
    margin = 4 * 1024 * 1024
    blocks = pl.pallas_call(
        functools.partial(place_kernel, strips, lanes),
        out_shape=jax.ShapeDtypeStruct((levels, lanes, CHUNKS, height, width), jnp.float32),
        in_specs=[smem] * 5 + [vmem] * 3,
        out_specs=vmem,
        scratch_shapes=[pltpu.VMEM((local, fh + 8 + 2 * height, fw), jnp.float32)],
        compiler_params=pltpu.CompilerParams(
            vmem_limit_bytes=(strips + 11 * local) * block_bytes + margin
        ),
    )(slots, row_anchor, col_anchor, first, end, corr_rows[None, :], corr_cols[None, :], residuals)
    stitched, power = pl.pallas_call(
        functools.partial(kernel, strips, lanes),
        out_shape=(
            jax.ShapeDtypeStruct((height, fw), jnp.float32),
            jax.ShapeDtypeStruct((1, fw), jnp.float32),
        ),
        in_specs=[smem] * 4 + [vmem],
        out_specs=(vmem, vmem),
        scratch_shapes=[
            pltpu.VMEM((height, fw), jnp.float32),
            pltpu.VMEM((others, levels, CHUNKS, height, width), jnp.float32),
            pltpu.VMEM((levels, CHUNKS, height, width), jnp.float32),
            pltpu.VMEM((2, levels, CHUNKS, height, width), jnp.float32),
            pltpu.VMEM((1, fw), jnp.float32),
            pltpu.VMEM((strips - 1, 1, fw), jnp.float32),
            dma((others, levels, CHUNKS)),
            dma((others, levels, CHUNKS)),
            dma((levels, CHUNKS)),
            dma((2, levels, CHUNKS)),
            dma((strips - 1,)),
            dma((strips - 1,)),
        ],
        compiler_params=pltpu.CompilerParams(
            collective_id=0,
            has_side_effects=True,
            vmem_limit_bytes=(2 * strips + 3 * levels + 4) * block_bytes + margin,
        ),
    )(row_anchor, col_anchor, first, end, blocks)
    return stitched, power[0]


def solution(mesh):
    strips = mesh.shape["strip"]
    lanes = math.gcd(strips, max(mesh.shape["col"] // 2, 1))
    in_specs = (P("strip", None, None), P(), P(), P(), P(), P(), P(), P())
    out_specs = (P("strip", "col"), P("col"))
    run = functools.partial(body, strips, lanes)
    return jax.shard_map(run, mesh=mesh, in_specs=in_specs, out_specs=out_specs, check_vma=False)
```

time: 128 us -> 38.8 us (0.30)
  waiting for transfers between devices: 58.7 us -> 0 us
  blocking collectives: 35.2 us -> 0 us
  Pallas kernels: 0 us -> 30.5 us
  between operations: 9.63 us -> 0.69 us
  starting transfers between devices: 7.41 us -> 0 us
  other arithmetic: 7.82 us -> 0.63 us
  matrix products: 1.64 us -> 0 us
    all_to_all x1 -> x0, waiting for transfers between devices: 58.7 us -> none  [body(): lax.all_to_all(num_send, 'strip', split_axis=0, concat_axis=0, tiled=True)]
    psum x1 -> x0, blocking collectives: 35.2 us -> none  [body(): column_sums = lax.psum(jnp.sum(stitched * stitched, axis=0), 'strip')]
    pallas_call x0 -> x2, Pallas kernels: none -> 30.5 us  [the longest x1 28.9 us: body(): pl.pallas_call(functools.partial(kernel, strips, lanes), out_shape=(jax.S...]
    all_to_all x1 -> x0, starting transfers between devices: 7.41 us -> none  [body(): lax.all_to_all(num_send, 'strip', split_axis=0, concat_axis=0, tiled=True)]
    unnamed x8 -> x23, local copies, waits for them, and re-layouts: 0.02 us -> 5.92 us
    dynamic_slice x3 -> x0, local copies, waits for them, and re-layouts: 4.14 us -> none  [the longest x1 1.41 us: body(): row_anchor[facet_id]]
    select_n x2 -> x0, other arithmetic: 2.63 us -> none  [body(): row_weight = jnp.where(inside, row_taper, 0.0)]
    dynamic_update_slice x2 -> x0, local copies, waits for them, and re-layouts: 2.36 us -> none  [body(): lax.dynamic_update_slice(canvas, shifted, (row_anchor[facet_id], 0))]
  transfers between devices with their start and end apart: 1 -> 0, of which waited for: 1 -> 0; matrix products, arithmetic and copies ran while one was open for 1% -> 0% of each run, Pallas kernels for 0% -> 0%
where the time goes in v1:
time: 38.8 us; the launch traced here: 38.5 us
  Pallas kernels  30.5 us (79%)
  local copies, waits for them, and re-layouts  6.64 us (17%)
  between operations  0.69 us (2%)
  other arithmetic  0.63 us (2%)
    pallas_call x1, Pallas kernels, body(): pl.pallas_call(functools.partial(kernel, strips, lanes), out_shape=(jax.S...  28.9 us
    unnamed x23, local copies, waits for them, and re-layouts  5.92 us
    pallas_call x1, Pallas kernels, body(): pl.pallas_call(functools.partial(place_kernel, strips, lanes), out_shape=...  1.69 us

profile of v1, /device:TPU:0, one launch (start us, length us, event | category | flops | bytes accessed | tf_op | source)
XLA Modules:
  0.0 38.5 jit_solution(14230430784501894634)
XLA Ops:
  0.6 0.7 %broadcast_in_dim.7.cols_ref = f32[1,2560]{1,0:T(1,128)S(1)} reshape(f32[2560]{0:T(1024)} %param.10) | data formatting | bytes 20480 | tf_op jit(solution)/shard_map/broadcast_in_dim | solution.py:248
  1.3 0.0 copy-start
  1.3 1.3 %copy-done = f32[2,64,2560]{2,1,0:T(8,128)S(1)} copy-done((f32[2,64,2560]{2,1,0:T(8,128)S(1)}, f32[2,64,2560]{2,1,0:T(8,128)}, u32[]{:S(2)}) %copy-start) | copy-done | bytes 1310744
  2.7 0.0 copy-start.1
  2.7 0.7 %copy-done.1 = s32[16]{0:T(128)S(1)} copy-done((s32[16]{0:T(128)S(1)}, s32[16]{0:T(128)}, u32[]{:S(2)}) %copy-start.1) | copy-done | bytes 88
  3.3 0.0 copy-start.3
  3.3 0.7 %copy-done.3 = s32[16]{0:T(128)S(1)} copy-done((s32[16]{0:T(128)S(1)}, s32[16]{0:T(128)}, u32[]{:S(2)}) %copy-start.3) | copy-done | bytes 88
  4.0 0.0 copy-start.5
  4.0 0.7 %copy-done.5 = s32[16]{0:T(128)S(1)} copy-done((s32[16]{0:T(128)S(1)}, s32[16]{0:T(128)}, u32[]{:S(2)}) %copy-start.5) | copy-done | bytes 88
  4.6 0.0 copy-start.7
  4.6 0.7 %copy-done.7 = s32[16]{0:T(128)S(1)} copy-done((s32[16]{0:T(128)S(1)}, s32[16]{0:T(128)}, u32[]{:S(2)}) %copy-start.7) | copy-done | bytes 88
  5.3 0.0 copy-start.9
  5.3 0.7 %copy-done.9 = s32[16]{0:T(128)S(1)} copy-done((s32[16]{0:T(128)S(1)}, s32[16]{0:T(128)}, u32[]{:S(2)}) %copy-start.9) | copy-done | bytes 88
  5.9 0.0 copy-start.10
  5.9 0.7 %copy-done.10 = f32[64]{0:T(128)S(1)} copy-done((f32[64]{0:T(128)S(1)}, f32[64]{0:T(128)}, u32[]{:S(2)}) %copy-start.10) | copy-done | bytes 280
  6.6 0.0 copy-start.2
  6.6 1.7 %shard_map.95.blocks_ref = f32[4,2,2,16,1280]{4,3,2,1,0:T(8,128)S(1)} custom-call(s32[16]{0:T(128)S(1)} %copy-done.9, s32[16]{0:T(128)S(1)} %copy-done.1, s32[16]{0:T(128)S(1)} %copy-done.3, s32[16]{0:T(128)S(1)} %copy-done.5, s32[16]{0:T(128)S(1)} %copy-done.7, f32[1,64]{1,0:T(1,128)S(1)} %bitcast.1, f32[1,2560]{1,0:T(1,128)S(1)} %broadcast_in_dim.7.cols_ref, ...), custom_call_target="tpu_custom_call" | custom-call | tf_op jit(solution)/shard_map/pallas_call | solution.py:239
  8.3 0.0 copy-done.2
  8.3 0.0 copy-done.4
  8.3 0.0 copy-done.6
  8.3 0.0 copy-done.8
  8.3 28.9 %shard_map.96 = (f32[16,2560]{1,0:T(8,128)S(1)}, f32[1,2560]{1,0:T(1,128)S(1)}) custom-call(s32[16]{0:T(128)S(1)} %copy-done.2, s32[16]{0:T(128)S(1)} %copy-done.4, s32[16]{0:T(128)S(1)} %copy-done.6, s32[16]{0:T(128)S(1)} %copy-done.8, f32[4,2,2,16,1280]{4,3,2,1,0:T(8,128)S(1)} %shard_map.95.blocks_ref), custom_call_target="tpu_custom_call" | custom-call | tf_op jit(solution)/shard_map/pallas_call | solution.py:249
  37.2 0.6 %reduce = f32[2560]{0:T(1024)} reduce(f32[1,2560]{1,0:T(1,128)S(1)} %get-tuple-element.5, f32[]{:T(128)} %constant.1), dimensions={0}, to_apply=%get-tuple-element.5.reduce_sub_computation | reduce | bytes 20484 | tf_op jit(solution)/shard_map/pallas_call | solution.py:249
  37.8 0.7 %copy.11 = f32[16,2560]{1,0:T(8,128)} copy(f32[16,2560]{1,0:T(8,128)S(1)} %get-tuple-element.8) | data formatting | bytes 327680
  (3 shorter events, 0.0 us)
Async XLA Ops:
  1.3 1.3 %copy-start = (f32[2,64,2560]{2,1,0:T(8,128)S(1)}, f32[2,64,2560]{2,1,0:T(8,128)}, u32[]{:S(2)}) copy-start(f32[2,64,2560]{2,1,0:T(8,128)} %res_ref.1) | copy-start | bytes 3932164
  2.7 0.7 %copy-start.1 = (s32[16]{0:T(128)S(1)}, s32[16]{0:T(128)}, u32[]{:S(2)}) copy-start(s32[16]{0:T(128)} %ra_ref.3) | copy-start | bytes 196
  3.3 0.7 %copy-start.3 = (s32[16]{0:T(128)S(1)}, s32[16]{0:T(128)}, u32[]{:S(2)}) copy-start(s32[16]{0:T(128)} %ca_ref.3) | copy-start | bytes 196
  4.0 0.7 %copy-start.5 = (s32[16]{0:T(128)S(1)}, s32[16]{0:T(128)}, u32[]{:S(2)}) copy-start(s32[16]{0:T(128)} %vf_ref.3) | copy-start | bytes 196
  4.6 0.7 %copy-start.7 = (s32[16]{0:T(128)S(1)}, s32[16]{0:T(128)}, u32[]{:S(2)}) copy-start(s32[16]{0:T(128)} %ve_ref.3) | copy-start | bytes 196
  5.3 0.7 %copy-start.9 = (s32[16]{0:T(128)S(1)}, s32[16]{0:T(128)}, u32[]{:S(2)}) copy-start(s32[16]{0:T(128)} %fid_ref.1) | copy-start | bytes 196
  5.9 0.7 %copy-start.10 = (f32[64]{0:T(128)S(1)}, f32[64]{0:T(128)}, u32[]{:S(2)}) copy-start(f32[64]{0:T(128)} %param.9) | copy-start | bytes 772
  6.6 1.7 %copy-start.2 = (s32[16]{0:T(128)S(1)}, s32[16]{0:T(128)}, u32[]{:S(2)}) copy-start(s32[16]{0:T(128)} %ra_ref.3) | copy-start | bytes 196
  6.6 1.7 %copy-start.4 = (s32[16]{0:T(128)S(1)}, s32[16]{0:T(128)}, u32[]{:S(2)}) copy-start(s32[16]{0:T(128)} %ca_ref.3) | copy-start | bytes 196
  6.6 1.7 %copy-start.6 = (s32[16]{0:T(128)S(1)}, s32[16]{0:T(128)}, u32[]{:S(2)}) copy-start(s32[16]{0:T(128)} %vf_ref.3) | copy-start | bytes 196
  6.6 1.7 %copy-start.8 = (s32[16]{0:T(128)S(1)}, s32[16]{0:T(128)}, u32[]{:S(2)}) copy-start(s32[16]{0:T(128)} %ve_ref.3) | copy-start | bytes 196

commit v2 on v1

v2 whole, which is shorter than its diff:
```python
import functools
import math

import jax
import jax.numpy as jnp
from jax import lax
from jax.experimental import pallas as pl
from jax.experimental.pallas import tpu as pltpu
from jax.sharding import PartitionSpec as P

MESH = pl.DeviceIdType.MESH
CHUNKS = 2


def taper(position, count):
    angle = (position.astype(jnp.float32) + (0.5 - count / 2)) * (math.pi / count)
    square = angle * angle
    value = jnp.full_like(square, 1.0 / math.factorial(12))
    for order in (10, 8, 6, 4, 2, 0):
        sign = -1.0 if order % 4 == 2 else 1.0
        value = value * square + sign / math.factorial(order)
    return value * value


def visit_order(count):
    return [sorted(range(count), key=lambda d: (-abs(d - z), d < z)) for z in range(count)]


def place_kernel(
    strips, lanes, fid_hbm, ra_hbm, ca_hbm, vf_hbm, ve_hbm, rows_hbm, cols_hbm, res_hbm,
    own_ref, send_ref, fid_ref, ra_ref, ca_ref, vf_ref, ve_ref, rows_ref, cols_ref, res_ref,
    placed, sems,
):
    local, fh, fw = res_ref.shape
    height = fh // 4
    width = fw // CHUNKS
    levels = strips // lanes
    share = local // 2
    strip = lax.axis_index("strip")
    group = lax.axis_index("col")
    x = lax.rem(strip, lanes)
    core = lax.rem(group, 2)

    small = [
        (fid_hbm, fid_ref), (ra_hbm, ra_ref), (ca_hbm, ca_ref), (vf_hbm, vf_ref),
        (ve_hbm, ve_ref), (rows_hbm, rows_ref), (cols_hbm, cols_ref),
    ]
    loads = [pltpu.make_async_copy(a, b, sems.at[i]) for i, (a, b) in enumerate(small)]
    facet_loads = [
        pltpu.make_async_copy(res_hbm.at[p], res_ref.at[p], sems.at[len(small) + p])
        for p in range(local)
    ]
    for load in loads + facet_loads:
        load.start()
    blank = jnp.zeros((height, fw), jnp.float32)
    for p in range(local):
        placed[p, pl.ds(0, height), :] = blank
        placed[p, pl.ds(height + fh + 8, height), :] = blank
    y = lax.broadcasted_iota(jnp.int32, (fh, 1), 0)
    u = lax.broadcasted_iota(jnp.int32, (1, fw), 1)
    sub = lax.broadcasted_iota(jnp.int32, (8, 1), 0)
    row_taper = taper(y, fh)
    col_taper = taper(u, fw)
    eye = lax.broadcasted_iota(jnp.int32, (fh, fh), 0) == lax.broadcasted_iota(
        jnp.int32, (fh, fh), 1
    )
    for load in loads:
        load.wait()
    corr_row = jnp.sum(jnp.where(eye, rows_ref[...], 0.0), axis=1, keepdims=True)
    corr_col = jnp.concatenate([cols_ref[pl.ds(i, 1), :] for i in range(fw // 128)], axis=1)
    col_scale = col_taper * corr_col
    tiles, masks = [], []
    for p in range(local):
        f = fid_ref[strip * local + p]
        ra, ca = ra_ref[f], ca_ref[f]
        inside = (y >= vf_ref[f]) & (y < ve_ref[f])
        row_scale = jnp.where(inside, row_taper, 0.0) * corr_row
        col_pos = u + (group * fw - ca)
        masks.append((col_pos >= 0) & (col_pos < fw))
        shift = lax.rem(ca, fw)
        lift = lax.rem(ra, 8)
        tiles.append(lax.div(ra, 8))
        held = jnp.zeros((8, fw), jnp.float32)
        facet_loads[p].wait()
        for row in range(0, fh, 8):
            term = res_ref[p, pl.ds(row, 8), :] * col_scale * row_scale[row : row + 8]
            term = pltpu.roll(pltpu.roll(term, shift, axis=1), lift, axis=0)
            placed[p, pl.ds(height + row, 8), :] = jnp.where(sub < lift, held, term)
            held = term
        placed[p, pl.ds(height + fh, 8), :] = jnp.where(sub < lift, held, 0.0)

    def rows_of(p, tile, block, columns):
        start = block * (height // 8) - tile
        start = (jnp.clip(start, -height // 8, fh // 8 + 1) + height // 8) * 8
        return placed[p, pl.ds(pl.multiple_of(start, 8), height), columns]

    for c in range(CHUNKS):
        columns = pl.ds(c * width, width)
        for h in range(share):
            p = core * share + h
            tile = lax.div(ra_ref[fid_ref[strip * local + p]], 8)
            for i in range(lanes - 1):
                for k in range(4 // lanes):
                    residue = lax.rem(x + i + 1, lanes) + lanes * k
                    parts = [
                        rows_of(p, tile, residue + 4 * turn, columns)
                        for turn in range(strips // 4)
                    ]
                    send_ref[i, k, c, h] = sum(parts[1:], parts[0])
        for d in range(levels):
            total = jnp.zeros((height, width), jnp.float32)
            for p in range(local):
                part = rows_of(p, tiles[p], d * lanes + x, columns)
                total += jnp.where(masks[p][:, c * width : (c + 1) * width], part, 0.0)
            own_ref[d, c] = total


def kernel(
    strips, lanes, fid_ref, ra_ref, ca_ref, vf_ref, ve_ref, own_ref, send_ref,
    out_ref, power_ref, den, xrecv, zsend, zrecv, psend, precv,
    xs_sem, xr_sem, rs_sem, rr_sem, zs_sem, zr_sem, ps_sem, pr_sem,
):
    facets = ra_ref.shape[0]
    height, fw = out_ref.shape
    fh = 4 * height
    levels = strips // lanes
    turns = 4 // lanes
    width = fw // CHUNKS
    share = send_ref.shape[3]
    strip = lax.axis_index("strip")
    group = lax.axis_index("col")
    z, x = lax.div(strip, lanes), lax.rem(strip, lanes)
    core = lax.rem(group, 2)
    partner = group + 1 - 2 * core

    barrier = pltpu.get_barrier_semaphore()
    for k in range(1, strips):
        peer = lax.rem(strip + k, strips)
        pl.semaphore_signal(barrier, inc=1, device_id={"strip": peer}, device_id_type=MESH)
    pl.semaphore_signal(barrier, inc=1, device_id={"col": partner}, device_id_type=MESH)

    order = visit_order(levels)

    def dest(t):
        d = jnp.int32(order[0][t])
        for place_z in range(1, levels):
            d = jnp.where(z == place_z, jnp.int32(order[place_z][t]), d)
        return d

    def x_copy(i, k, c):
        return pltpu.make_async_remote_copy(
            src_ref=send_ref.at[i, k, c],
            dst_ref=xrecv.at[core, i, k, c],
            send_sem=xs_sem.at[i, k, c],
            recv_sem=xr_sem.at[i, k, c],
            device_id={"strip": z * lanes + lax.rem(x + i + 1, lanes)},
            device_id_type=MESH,
        )

    def relay(i, k, c):
        return pltpu.make_async_remote_copy(
            src_ref=xrecv.at[core, i, k, c],
            dst_ref=xrecv.at[core, i, k, c],
            send_sem=rs_sem.at[i, k, c],
            recv_sem=rr_sem.at[i, k, c],
            device_id={"col": partner},
            device_id_type=MESH,
        )

    def z_copy(way, d, c, target):
        return pltpu.make_async_remote_copy(
            src_ref=zsend.at[d, c],
            dst_ref=zrecv.at[way, d, c],
            send_sem=zs_sem.at[d, c],
            recv_sem=zr_sem.at[way, d, c],
            device_id={"strip": target * lanes + x},
            device_id_type=MESH,
        )

    def p_copy(k):
        return pltpu.make_async_remote_copy(
            src_ref=psend,
            dst_ref=precv.at[k - 1],
            send_sem=ps_sem.at[k - 1],
            recv_sem=pr_sem.at[k - 1],
            device_id={"strip": lax.rem(strip + k, strips)},
            device_id_type=MESH,
        )

    v = lax.broadcasted_iota(jnp.int32, (height, 1), 0)
    u8 = lax.broadcasted_iota(jnp.int32, (8, fw), 1) + group * fw
    den[...] = jnp.zeros_like(den)

    def add_facet(f, carry):
        row_pos = v + (strip * height - ra_ref[f])
        row_inside = (row_pos >= vf_ref[f]) & (row_pos < ve_ref[f])
        row_part = jnp.where(row_inside, taper(row_pos, fh), 0.0)
        col_pos = u8 - ca_ref[f]
        col_inside = (col_pos >= 0) & (col_pos < fw)
        col_part = jnp.where(col_inside, taper(col_pos, fw), 0.0)
        for row in range(0, height, 8):
            den[pl.ds(row, 8), :] += row_part[row : row + 8] * col_part
        return carry

    lax.fori_loop(0, facets, add_facet, 0)

    pl.semaphore_wait(barrier, strips)
    pairs = [(i, c) for c in range(CHUNKS) for i in range(lanes - 1)]
    turn = [lax.rem(dest(0) + kk, turns) for kk in range(turns)]
    for k in turn:
        for i, c in pairs:
            x_copy(i, k, c).start()

    def gather(d, c):
        total = own_ref[d, c]
        k = lax.rem(d, turns)
        u = lax.broadcasted_iota(jnp.int32, (1, width), 1) + (group * fw + c * width)
        for i in range(lanes - 1):
            source = z * lanes + lax.rem(x + lanes - i - 1, lanes)
            for p in range(2 * share):
                f = fid_ref[source * (2 * share) + p]
                row_pos = v + ((d * lanes + x) * height - ra_ref[f])
                col_pos = u - ca_ref[f]
                inside = (row_pos >= 0) & (row_pos < fh) & (col_pos >= 0) & (col_pos < fw)
                total += jnp.where(inside, xrecv[p // share, i, k, c, p % share], 0.0)
        return total

    def pass_on(k):
        for i, c in pairs:
            x_copy(i, k, c).wait_recv()
            relay(i, k, c).start()

    pass_on(turn[0])
    for i, c in pairs:
        relay(i, turn[0], c).wait_recv()
    for t in range(levels - 1):
        d = dest(t)
        right = d > z
        way = jnp.where(right, 0, 1)
        target = jnp.where(right, z + 1, z - 1)
        fed = jnp.where(right, z > 0, z < levels - 1)
        for c in range(CHUNKS):
            zsend[d, c] = gather(d, c)

            @pl.when(jnp.logical_not(fed))
            def _():
                z_copy(way, d, c, target).start()

        if t == 0:
            for k in turn[1:]:
                pass_on(k)
        for c in range(CHUNKS):

            @pl.when(fed)
            def _():
                z_copy(way, d, c, target).wait_recv()
                zsend[d, c] += zrecv[way, d, c]
                z_copy(way, d, c, target).start()

        if t == 0:
            for k in turn[1:]:
                for i, c in pairs:
                    relay(i, k, c).wait_recv()

    for c in range(CHUNKS):
        columns = pl.ds(c * width, width)
        out_ref[:, columns] = gather(z, c)
    for c in range(CHUNKS):
        columns = pl.ds(c * width, width)

        @pl.when(z > 0)
        def _():
            z_copy(0, z, c, z - 1).wait_recv()
            out_ref[:, columns] += zrecv[0, z, c]

        @pl.when(z < levels - 1)
        def _():
            z_copy(1, z, c, z + 1).wait_recv()
            out_ref[:, columns] += zrecv[1, z, c]

        stitched = out_ref[:, columns] / jnp.maximum(den[:, columns], 0.5)
        out_ref[:, columns] = stitched
        psend[:, columns] = jnp.sum(stitched * stitched, axis=0, keepdims=True)

    for k in range(1, strips):
        p_copy(k).start()
    total = psend[...]
    for k in range(1, strips):
        p_copy(k).wait_recv()
        total = total + precv[k - 1]
    total = total * (1.0 / (strips * height))
    for row in range(fw // 128):
        power_ref[pl.ds(row, 1), :] = total[:, row * 128 : (row + 1) * 128]

    for k in range(1, strips):
        p_copy(k).wait_send()
    for k in turn:
        for i, c in pairs:
            x_copy(i, k, c).wait_send()
            relay(i, k, c).wait_send()
    for t in range(levels - 1):
        d = dest(t)
        for c in range(CHUNKS):
            z_copy(0, d, c, jnp.where(d > z, z + 1, z - 1)).wait_send()


def body(strips, lanes, residuals, corr_rows, corr_cols, row_anchor, col_anchor, first, end, slots):
    local, fh, fw = residuals.shape
    height = fh // 4
    levels = strips // lanes
    turns = 4 // lanes
    share = local // 2
    width = fw // CHUNKS
    others = max(lanes - 1, 1)
    sent = (others, turns, CHUNKS, share, height, width)
    smem = pl.BlockSpec(memory_space=pltpu.SMEM)
    vmem = pl.BlockSpec(memory_space=pltpu.VMEM)
    hbm = pl.BlockSpec(memory_space=pltpu.HBM)
    dma = pltpu.SemaphoreType.DMA
    table = pltpu.SMEM(slots.shape, jnp.int32)
    block_bytes = 4 * height * fw
    margin = 4 * 1024 * 1024
    own, send = pl.pallas_call(
        functools.partial(place_kernel, strips, lanes),
        out_shape=(
            jax.ShapeDtypeStruct((levels, CHUNKS, height, width), jnp.float32),
            jax.ShapeDtypeStruct(sent, jnp.float32),
        ),
        in_specs=[hbm] * 8,
        out_specs=(vmem, vmem),
        scratch_shapes=[table] * 5
        + [
            pltpu.VMEM((1, fh), jnp.float32),
            pltpu.VMEM((fw // 128, 128), jnp.float32),
            pltpu.VMEM((local, fh, fw), jnp.float32),
            pltpu.VMEM((local, fh + 8 + 2 * height, fw), jnp.float32),
            dma((7 + local,)),
        ],
        compiler_params=pltpu.CompilerParams(
            vmem_limit_bytes=(strips + 14 * local) * block_bytes + margin
        ),
    )(
        slots, row_anchor, col_anchor, first, end,
        corr_rows[None, :], corr_cols.reshape(fw // 128, 128), residuals,
    )
    stitched, power = pl.pallas_call(
        functools.partial(kernel, strips, lanes),
        out_shape=(
            jax.ShapeDtypeStruct((height, fw), jnp.float32),
            jax.ShapeDtypeStruct((fw // 128, 128), jnp.float32),
        ),
        in_specs=[smem] * 5 + [vmem] * 2,
        out_specs=(vmem, vmem),
        scratch_shapes=[
            pltpu.VMEM((height, fw), jnp.float32),
            pltpu.VMEM((2,) + sent, jnp.float32),
            pltpu.VMEM((levels, CHUNKS, height, width), jnp.float32),
            pltpu.VMEM((2, levels, CHUNKS, height, width), jnp.float32),
            pltpu.VMEM((1, fw), jnp.float32),
            pltpu.VMEM((strips - 1, 1, fw), jnp.float32),
            dma((others, turns, CHUNKS)),
            dma((others, turns, CHUNKS)),
            dma((others, turns, CHUNKS)),
            dma((others, turns, CHUNKS)),
            dma((levels, CHUNKS)),
            dma((2, levels, CHUNKS)),
            dma((strips - 1,)),
            dma((strips - 1,)),
        ],
        compiler_params=pltpu.CompilerParams(
            collective_id=0,
            has_side_effects=True,
            vmem_limit_bytes=(2 * strips + 4 * levels + 16) * block_bytes + margin,
        ),
    )(slots, row_anchor, col_anchor, first, end, own, send)
    return stitched, power.reshape(fw)


def solution(mesh):
    strips = mesh.shape["strip"]
    lanes = math.gcd(strips, max(mesh.shape["col"] // 2, 1))
    in_specs = (P("strip", None, None), P(), P(), P(), P(), P(), P(), P())
    out_specs = (P("strip", "col"), P("col"))
    run = functools.partial(body, strips, lanes)
    return jax.shard_map(run, mesh=mesh, in_specs=in_specs, out_specs=out_specs, check_vma=False)
```

time: 38.8 us -> 41.5 us (1.070)
  Pallas kernels: 30.5 us -> 33.2 us
  other arithmetic: 0.63 us -> 0 us
  local copies, waits for them, and re-layouts: 6.64 us -> 7.26 us
    pallas_call x1, Pallas kernels: 28.9 us -> 31.8 us  [body(): pl.pallas_call(functools.partial(kernel, strips, lanes), out_shape=(jax.S...]
    unnamed x23 -> x28, local copies, waits for them, and re-layouts: 5.92 us -> 7.26 us
    broadcast_in_dim x1 -> x0, local copies, waits for them, and re-layouts: 0.72 us -> none  [body(): corr_cols[None, :]]
    pallas_call x1 -> x0, other arithmetic: 0.63 us -> none  [body(): pl.pallas_call(functools.partial(kernel, strips, lanes), out_shape=(jax.S...]
where the time goes in v2:
time: 41.5 us; the launch traced here: 41.2 us
  Pallas kernels  33.2 us (80%)
  local copies, waits for them, and re-layouts  7.26 us (17%)
  between operations  0.74 us (2%)
    pallas_call x1, Pallas kernels, body(): pl.pallas_call(functools.partial(kernel, strips, lanes), out_shape=(jax.S...  31.8 us
    unnamed x28, local copies, waits for them, and re-layouts  7.26 us
    pallas_call x1, Pallas kernels, body(): pl.pallas_call(functools.partial(place_kernel, strips, lanes), out_shape=...  1.47 us

profile of v2, /device:TPU:0, one launch (start us, length us, event | category | flops | bytes accessed | tf_op | source)
XLA Modules:
  0.0 41.2 jit_solution(6304814586021723202)
XLA Ops:
  0.6 0.0 copy-start.3
  0.6 0.0 copy-start.11
  0.7 0.0 copy-start.9
  0.7 0.0 copy-start.7
  0.7 0.0 copy-start.5
  0.7 0.0 copy-start
  0.7 1.3 %copy-done = f32[2,64,2560]{2,1,0:T(8,128)S(1)} copy-done((f32[2,64,2560]{2,1,0:T(8,128)S(1)}, f32[2,64,2560]{2,1,0:T(8,128)}, u32[]{:S(2)}) %copy-start) | copy-done | bytes 1310744
  2.0 0.0 copy-start.1
  2.0 0.7 %copy-done.1 = f32[2560]{0:T(1024)S(1)} copy-done((f32[2560]{0:T(1024)S(1)}, f32[2560]{0:T(1024)}, u32[]{:S(2)}) %copy-start.1) | copy-done | bytes 10264
  2.7 0.7 %copy-done.2 = s32[16]{0:T(128)S(1)} copy-done((s32[16]{0:T(128)S(1)}, s32[16]{0:T(128)}, u32[]{:S(2)}) %copy-start.2) | copy-done | bytes 88
  3.4 0.7 %copy-done.4 = s32[16]{0:T(128)S(1)} copy-done((s32[16]{0:T(128)S(1)}, s32[16]{0:T(128)}, u32[]{:S(2)}) %copy-start.4) | copy-done | bytes 88
  4.0 0.7 %copy-done.6 = s32[16]{0:T(128)S(1)} copy-done((s32[16]{0:T(128)S(1)}, s32[16]{0:T(128)}, u32[]{:S(2)}) %copy-start.6) | copy-done | bytes 88
  4.7 0.7 %copy-done.8 = s32[16]{0:T(128)S(1)} copy-done((s32[16]{0:T(128)S(1)}, s32[16]{0:T(128)}, u32[]{:S(2)}) %copy-start.8) | copy-done | bytes 88
  5.4 0.7 %copy-done.10 = s32[16]{0:T(128)S(1)} copy-done((s32[16]{0:T(128)S(1)}, s32[16]{0:T(128)}, u32[]{:S(2)}) %copy-start.10) | copy-done | bytes 88
  6.0 0.7 %copy-done.12 = f32[64]{0:T(128)S(1)} copy-done((f32[64]{0:T(128)S(1)}, f32[64]{0:T(128)}, u32[]{:S(2)}) %copy-start.12) | copy-done | bytes 280
  6.7 1.5 %shard_map.95 = (f32[4,2,16,1280]{3,2,1,0:T(8,128)S(1)}, f32[1,2,2,1,16,1280]{5,4,3,2,1,0:T(8,128)S(1)}) custom-call(s32[16]{0:T(128)S(1)} %copy-done.2, s32[16]{0:T(128)S(1)} %copy-done.4, s32[16]{0:T(128)S(1)} %copy-done.6, s32[16]{0:T(128)S(1)} %copy-done.8, s32[16]{0:T(128)S(1)} %copy-done.10, f32[1,64]{1,0:T(1,128)S(1)} %bitcast.5, ...), custom_call_target="tpu_custom_call" | custom-call | tf_op jit(solution)/shard_map/pallas_call | solution.py:323
  8.1 0.0 copy-done.3
  8.2 0.0 copy-done.11
  8.2 0.0 copy-done.9
  8.2 0.0 copy-done.7
  8.2 0.0 copy-done.5
  8.2 31.8 %shard_map.96 = (f32[16,2560]{1,0:T(8,128)S(1)}, f32[20,128]{1,0:T(8,128)S(1)}) custom-call(s32[16]{0:T(128)S(1)} %copy-done.3, s32[16]{0:T(128)S(1)} %copy-done.5, s32[16]{0:T(128)S(1)} %copy-done.7, s32[16]{0:T(128)S(1)} %copy-done.9, s32[16]{0:T(128)S(1)} %copy-done.11, f32[4,2,16,1280]{3,2,1,0:T(8,128)S(1)} %get-tuple-element.6.own_ref, ...), custom_call_target="tpu_custom_call" | custom-call | tf_op jit(solution)/shard_map/pallas_call | solution.py:346
  40.0 0.7 %copy.12 = f32[16,2560]{1,0:T(8,128)} copy(f32[16,2560]{1,0:T(8,128)S(1)} %get-tuple-element.12) | data formatting | bytes 327680
  40.6 0.6 %copy.13 = f32[2560]{0:T(1024)} copy(f32[2560]{0:T(1024)S(1)} %bitcast.4) | data formatting | bytes 20480
  (6 shorter events, 0.0 us)
Async XLA Ops:
  0.6 7.5 %copy-start.3 = (s32[16]{0:T(128)S(1)}, s32[16]{0:T(128)}, u32[]{:S(2)}) copy-start(s32[16]{0:T(128)} %fid_ref.1) | copy-start | bytes 196
  0.6 7.5 %copy-start.11 = (s32[16]{0:T(128)S(1)}, s32[16]{0:T(128)}, u32[]{:S(2)}) copy-start(s32[16]{0:T(128)} %ve_ref.1) | copy-start | bytes 196
  0.7 7.5 %copy-start.9 = (s32[16]{0:T(128)S(1)}, s32[16]{0:T(128)}, u32[]{:S(2)}) copy-start(s32[16]{0:T(128)} %vf_ref.1) | copy-start | bytes 196
  0.7 7.5 %copy-start.7 = (s32[16]{0:T(128)S(1)}, s32[16]{0:T(128)}, u32[]{:S(2)}) copy-start(s32[16]{0:T(128)} %ca_ref.1) | copy-start | bytes 196
  0.7 7.5 %copy-start.5 = (s32[16]{0:T(128)S(1)}, s32[16]{0:T(128)}, u32[]{:S(2)}) copy-start(s32[16]{0:T(128)} %ra_ref.1) | copy-start | bytes 196
  0.7 1.3 %copy-start = (f32[2,64,2560]{2,1,0:T(8,128)S(1)}, f32[2,64,2560]{2,1,0:T(8,128)}, u32[]{:S(2)}) copy-start(f32[2,64,2560]{2,1,0:T(8,128)} %res_hbm.1) | copy-start | bytes 3932164
  2.0 0.7 %copy-start.1 = (f32[2560]{0:T(1024)S(1)}, f32[2560]{0:T(1024)}, u32[]{:S(2)}) copy-start(f32[2560]{0:T(1024)} %param.10) | copy-start | bytes 30724
  2.7 0.7 %copy-start.2 = (s32[16]{0:T(128)S(1)}, s32[16]{0:T(128)}, u32[]{:S(2)}) copy-start(s32[16]{0:T(128)} %fid_ref.1) | copy-start | bytes 196
  3.4 0.7 %copy-start.4 = (s32[16]{0:T(128)S(1)}, s32[16]{0:T(128)}, u32[]{:S(2)}) copy-start(s32[16]{0:T(128)} %ra_ref.1) | copy-start | bytes 196
  4.0 0.7 %copy-start.6 = (s32[16]{0:T(128)S(1)}, s32[16]{0:T(128)}, u32[]{:S(2)}) copy-start(s32[16]{0:T(128)} %ca_ref.1) | copy-start | bytes 196
  4.7 0.7 %copy-start.8 = (s32[16]{0:T(128)S(1)}, s32[16]{0:T(128)}, u32[]{:S(2)}) copy-start(s32[16]{0:T(128)} %vf_ref.1) | copy-start | bytes 196
  5.4 0.7 %copy-start.10 = (s32[16]{0:T(128)S(1)}, s32[16]{0:T(128)}, u32[]{:S(2)}) copy-start(s32[16]{0:T(128)} %ve_ref.1) | copy-start | bytes 196
  6.0 0.7 %copy-start.12 = (f32[64]{0:T(128)S(1)}, f32[64]{0:T(128)}, u32[]{:S(2)}) copy-start(f32[64]{0:T(128)} %param.9) | copy-start | bytes 772

commit v3 on v2

--- a/solution.py
+++ b/solution.py
@@ -9,7 +9,8 @@
 from jax.sharding import PartitionSpec as P
 
 MESH = pl.DeviceIdType.MESH
-CHUNKS = 2
+CHUNKS = 4
+VMEM_BYTES = 67043328
 
 
 def taper(position, count):
@@ -116,8 +117,9 @@
 
 
 def kernel(
-    strips, lanes, fid_ref, ra_ref, ca_ref, vf_ref, ve_ref, own_ref, send_ref,
-    out_ref, power_ref, den, xrecv, zsend, zrecv, psend, precv,
+    strips, lanes, fid_hbm, ra_hbm, ca_hbm, vf_hbm, ve_hbm, own_hbm, send_hbm,
+    out_ref, power_ref, fid_ref, ra_ref, ca_ref, vf_ref, ve_ref, own_ref, send_ref, load_sem,
+    den, xrecv, zsend, zrecv, psend, precv,
     xs_sem, xr_sem, rs_sem, rr_sem, zs_sem, zr_sem, ps_sem, pr_sem,
 ):
     facets = ra_ref.shape[0]
@@ -187,8 +189,27 @@
             device_id_type=MESH,
         )
 
+    sources = (fid_hbm, ra_hbm, ca_hbm, vf_hbm, ve_hbm, own_hbm, send_hbm)
+    targets = (fid_ref, ra_ref, ca_ref, vf_ref, ve_ref, own_ref, send_ref)
+    loads = [
+        pltpu.make_async_copy(a, b, load_sem.at[i])
+        for i, (a, b) in enumerate(zip(sources, targets))
+    ]
+    for load in loads:
+        load.start()
+
+    loads[6].wait()
+    pl.semaphore_wait(barrier, strips)
+    pairs = [(i, c) for c in range(CHUNKS) for i in range(lanes - 1)]
+    turn = [lax.rem(dest(0) + kk, turns) for kk in range(turns)]
+    for k in turn:
+        for i, c in pairs:
+            x_copy(i, k, c).start()
+
     v = lax.broadcasted_iota(jnp.int32, (height, 1), 0)
     u8 = lax.broadcasted_iota(jnp.int32, (8, fw), 1) + group * fw
+    for load in loads[:6]:
+        load.wait()
     den[...] = jnp.zeros_like(den)
 
     def add_facet(f, carry):
@@ -203,13 +224,6 @@
         return carry
 
     lax.fori_loop(0, facets, add_facet, 0)
-
-    pl.semaphore_wait(barrier, strips)
-    pairs = [(i, c) for c in range(CHUNKS) for i in range(lanes - 1)]
-    turn = [lax.rem(dest(0) + kk, turns) for kk in range(turns)]
-    for k in turn:
-        for i, c in pairs:
-            x_copy(i, k, c).start()
 
     def gather(d, c):
         total = own_ref[d, c]
@@ -225,31 +239,38 @@
                 total += jnp.where(inside, xrecv[p // share, i, k, c, p % share], 0.0)
         return total
 
-    def pass_on(k):
-        for i, c in pairs:
+    def pass_on(k, c):
+        for i in range(lanes - 1):
             x_copy(i, k, c).wait_recv()
             relay(i, k, c).start()
 
-    pass_on(turn[0])
-    for i, c in pairs:
-        relay(i, turn[0], c).wait_recv()
+    def passed(k, c):
+        for i in range(lanes - 1):
+            relay(i, k, c).wait_recv()
+
     for t in range(levels - 1):
         d = dest(t)
         right = d > z
         way = jnp.where(right, 0, 1)
         target = jnp.where(right, z + 1, z - 1)
         fed = jnp.where(right, z > 0, z < levels - 1)
+        if t == 0:
+            pass_on(turn[0], 0)
         for c in range(CHUNKS):
+            if t == 0:
+                if c + 1 < CHUNKS:
+                    pass_on(turn[0], c + 1)
+                passed(turn[0], c)
             zsend[d, c] = gather(d, c)
 
             @pl.when(jnp.logical_not(fed))
             def _():
                 z_copy(way, d, c, target).start()
 
-        if t == 0:
-            for k in turn[1:]:
-                pass_on(k)
         for c in range(CHUNKS):
+            if t == 0:
+                for k in turn[1:]:
+                    pass_on(k, c)
 
             @pl.when(fed)
             def _():
@@ -259,8 +280,8 @@
 
         if t == 0:
             for k in turn[1:]:
-                for i, c in pairs:
-                    relay(i, k, c).wait_recv()
+                for c in range(CHUNKS):
+                    passed(k, c)
 
     for c in range(CHUNKS):
         columns = pl.ds(c * width, width)
@@ -313,13 +334,10 @@
     width = fw // CHUNKS
     others = max(lanes - 1, 1)
     sent = (others, turns, CHUNKS, share, height, width)
-    smem = pl.BlockSpec(memory_space=pltpu.SMEM)
     vmem = pl.BlockSpec(memory_space=pltpu.VMEM)
     hbm = pl.BlockSpec(memory_space=pltpu.HBM)
     dma = pltpu.SemaphoreType.DMA
     table = pltpu.SMEM(slots.shape, jnp.int32)
-    block_bytes = 4 * height * fw
-    margin = 4 * 1024 * 1024
     own, send = pl.pallas_call(
         functools.partial(place_kernel, strips, lanes),
         out_shape=(
@@ -337,7 +355,7 @@
             dma((7 + local,)),
         ],
         compiler_params=pltpu.CompilerParams(
-            vmem_limit_bytes=(strips + 14 * local) * block_bytes + margin
+            vmem_limit_bytes=VMEM_BYTES
         ),
     )(
         slots, row_anchor, col_anchor, first, end,
@@ -349,9 +367,13 @@
             jax.ShapeDtypeStruct((height, fw), jnp.float32),
             jax.ShapeDtypeStruct((fw // 128, 128), jnp.float32),
         ),
-        in_specs=[smem] * 5 + [vmem] * 2,
+        in_specs=[hbm] * 7,
         out_specs=(vmem, vmem),
         scratch_shapes=[
+            *[table] * 5,
+            pltpu.VMEM((levels, CHUNKS, height, width), jnp.float32),
+            pltpu.VMEM(sent, jnp.float32),
+            dma((7,)),
             pltpu.VMEM((height, fw), jnp.float32),
             pltpu.VMEM((2,) + sent, jnp.float32),
             pltpu.VMEM((levels, CHUNKS, height, width), jnp.float32),
@@ -370,7 +392,7 @@
         compiler_params=pltpu.CompilerParams(
             collective_id=0,
             has_side_effects=True,
-            vmem_limit_bytes=(2 * strips + 4 * levels + 16) * block_bytes + margin,
+            vmem_limit_bytes=VMEM_BYTES,
         ),
     )(slots, row_anchor, col_anchor, first, end, own, send)
     return stitched, power.reshape(fw)

time: 41.5 us -> 37.6 us (0.906)
  local copies, waits for them, and re-layouts: 7.26 us -> 2.9 us
  Pallas kernels: 33.2 us -> 33.8 us
    unnamed x28 -> x2, local copies, waits for them, and re-layouts: 7.26 us -> 2.9 us
    pallas_call x1, Pallas kernels: 1.47 us -> 2.87 us  [body(): pl.pallas_call(functools.partial(place_kernel, strips, lanes), out_shape=...]
    pallas_call x1, Pallas kernels: 31.8 us -> 31 us  [body(): pl.pallas_call(functools.partial(kernel, strips, lanes), out_shape=(jax.S...]
where the time goes in v3:
time: 37.6 us; the launch traced here: 37.4 us
  Pallas kernels  33.8 us (90%)
  local copies, waits for them, and re-layouts  2.9 us (8%)
  between operations  0.65 us (2%)
    pallas_call x1, Pallas kernels, body(): pl.pallas_call(functools.partial(kernel, strips, lanes), out_shape=(jax.S...  31 us
    unnamed x2, local copies, waits for them, and re-layouts  2.9 us
    pallas_call x1, Pallas kernels, body(): pl.pallas_call(functools.partial(place_kernel, strips, lanes), out_shape=...  2.87 us

profile of v3, /device:TPU:0, one launch (start us, length us, event | category | flops | bytes accessed | tf_op | source)
XLA Modules:
  0.0 37.4 jit_solution(2330829373706528202)
XLA Ops:
  0.6 2.9 %shard_map.95 = (f32[4,4,16,640]{3,2,1,0:T(8,128)}, f32[1,2,4,1,16,640]{5,4,3,2,1,0:T(8,128)}) custom-call(s32[16]{0:T(128)} %fid_hbm.3, s32[16]{0:T(128)} %ra_hbm.3, s32[16]{0:T(128)} %ca_hbm.3, s32[16]{0:T(128)} %vf_hbm.3, s32[16]{0:T(128)} %ve_hbm.3, f32[1,64]{1,0:T(1,128)} %bitcast.5, f32[20,128]{1,0:T(8,128)} %bitcast.3, f32[2,64,2560]{2,1,0:T(8,128)} %res_hbm.1), custom_call_target="tpu_custom_call" | custom-call | tf_op jit(solution)/shard_map/pallas_call | solution.py:341
  3.5 31.0 %shard_map.96 = (f32[16,2560]{1,0:T(8,128)}, f32[20,128]{1,0:T(8,128)}) custom-call(s32[16]{0:T(128)} %fid_hbm.3, s32[16]{0:T(128)} %ra_hbm.3, s32[16]{0:T(128)} %ca_hbm.3, s32[16]{0:T(128)} %vf_hbm.3, s32[16]{0:T(128)} %ve_hbm.3, f32[4,4,16,640]{3,2,1,0:T(8,128)} %get-tuple-element.6.own_hbm, f32[1,2,4,1,16,640]{5,4,3,2,1,0:T(8,128)} %get-tuple-element.7.send_hbm), custom_call_target="tpu_custom_call" | custom-call | tf_op jit(solution)/shard_map/pallas_call | solution.py:364
  34.5 1.6 %copy.12 = f32[16,2560]{1,0:T(8,128)} copy(f32[16,2560]{1,0:T(8,128)} %get-tuple-element.12) | data formatting | bytes 327680
  36.1 1.3 %copy.13 = f32[2560]{0:T(1024)} copy(f32[2560]{0:T(1024)} %bitcast.4) | data formatting | bytes 20480
